TPU v7x, 32 devices: a whole 2x2x4 slice. The times are simulated.
32 devices in a mesh: dp: 16 (over z, x, core), seq: 2 (over y).
Axes of the slice: x: 2, y: 2, z: 4, core: 2. Of those that a mesh axis runs over, the one named last changes fastest.
Arguments:
- tokens: float32 [16384, 1024], P(('dp', 'seq')), may hold values from -6 to 6
- lengths: int32 [16, 1], P('dp'), may hold values from 1024 to 1024, as said below
- attn_gain: bfloat16 [1024], P('dp'), may hold values from 0.5 to 1.5
- w_query: bfloat16 [1024, 1024], P('dp'), may hold values from -0.1875 to 0.1875
- w_key: bfloat16 [1024, 512], P('dp'), may hold values from -0.1875 to 0.1875
- w_value: bfloat16 [1024, 512], P('dp'), may hold values from -0.1875 to 0.1875
- query_gain: bfloat16 [64], P('dp'), may hold values from 1 to 2
- key_gain: bfloat16 [64], P('dp'), may hold values from 0.5 to 1.5
- w_out: bfloat16 [1024, 1024], P('dp'), may hold values from -1.5 to 1.5
- ffn_gain: bfloat16 [1024], P('dp'), may hold values from 0.5 to 1.5
- w_gate: bfloat16 [1024, 4608], P('dp'), may hold values from -0.1875 to 0.1875
- w_up: bfloat16 [1024, 4608], P('dp'), may hold values from -0.1875 to 0.1875
- w_down: bfloat16 [4608, 1024], P('dp'), may hold values from -0.09375 to 0.09375
- cotangent: float32 [16384, 1024], P(('dp', 'seq')), may hold values from -6 to 6
Outputs:
- block_out: float32 [16384, 1024], P(('dp', 'seq'))
- d_tokens: float32 [16384, 1024], P(('dp', 'seq'))
- d_attn_gain: float32 [1024], P('dp')
- d_w_query: float32 [1024, 1024], P('dp')
- d_w_key: float32 [1024, 512], P('dp')
- d_w_value: float32 [1024, 512], P('dp')
- d_query_gain: float32 [64], P('dp')
- d_key_gain: float32 [64], P('dp')
- d_w_out: float32 [1024, 1024], P('dp')
- d_ffn_gain: float32 [1024], P('dp')
- d_w_gate: float32 [1024, 4608], P('dp')
- d_w_up: float32 [1024, 4608], P('dp')
- d_w_down: float32 [4608, 1024], P('dp')
Inputs may be any that keep to these rules, and one draw needn't show every extreme that they name: `lengths`: every length is at least 1024; in every draw one pack, drawn from the seed, has every sequence of length 1024 and no padding.
All inputs are finite; a program needn't handle non-finite values.
Results may differ from a plain program's by a relative error of at most 0.02.
Values may be sent and summed in bfloat16 or wider, within the bound.
No kernel may reach another device: no remote copies, remote signals or barrier semaphores. Data moves between devices by JAX's collectives and lax.ppermute only.
A program may use at most 192 MiB of HBM per device.

v0:
```python
from functools import partial
import math
import jax
import jax.numpy as jnp
from jax import lax
from jax.sharding import PartitionSpec as P

H = 16
KV = 8
HD = 64
EPSILON = 1e-05
ROPE_BASE = 1000000.0
MASKED_SCORE = -1e30


def rms_norm(values, gain_vec):
    return (
        values * lax.rsqrt(jnp.mean(values * values, axis=-1, keepdims=True) + EPSILON) * gain_vec
    )


def rope_tables(positions, head_size):
    half_size = head_size // 2
    freqs = ROPE_BASE ** (-(jnp.arange(half_size, dtype=jnp.float32) * (2.0 / head_size)))
    angles = positions.astype(jnp.float32)[:, None] * freqs[None, :]
    return (jnp.cos(angles), jnp.sin(angles))


def rotate(values, cos_tab, sin_tab):
    half_size = values.shape[-1] // 2
    first = values[..., :half_size]
    second = values[..., half_size:]
    cos_b = cos_tab[:, None, :]
    sin_b = sin_tab[:, None, :]
    return jnp.concatenate(
        [first * cos_b - second * sin_b, second * cos_b + first * sin_b], axis=-1
    )


def qk_prep(linear, gain_vec, cos_tab, sin_tab, heads):
    shaped = linear.reshape(linear.shape[0], heads, -1)
    return rotate(rms_norm(shaped, gain_vec), cos_tab, sin_tab)


def swiglu(gate_act, up_act):
    return jax.nn.silu(gate_act) * up_act


def pack_layout(seq_lens, total):
    places = jnp.arange(total, dtype=jnp.int32)
    ends = jnp.cumsum(seq_lens)
    starts = ends - seq_lens
    segment = jnp.sum((places[:, None] >= ends[None, :]).astype(jnp.int32), axis=1)
    starts_ext = jnp.concatenate([starts, ends[-1:]])
    labels = jnp.arange(seq_lens.shape[0] + 1, dtype=jnp.int32)
    offset = jnp.sum(jnp.where(segment[:, None] == labels[None, :], starts_ext[None, :], 0), axis=1)
    return (places, segment, places - offset, segment < seq_lens.shape[0])


def mat_dot(form, left, right):
    return jnp.einsum(form, left, right, preferred_element_type=jnp.float32)


def body(
    tokens,
    lengths,
    attn_gain,
    w_query,
    w_key,
    w_value,
    query_gain,
    key_gain,
    w_out,
    ffn_gain,
    w_gate,
    w_up,
    w_down,
    cotangent,
):
    seq_count = lax.axis_size("seq")
    seq_rank = lax.axis_index("seq")
    tok_rows = tokens.shape[0]
    pack_len = tok_rows * seq_count
    local_kv = KV // seq_count
    group = H // KV
    local_q = local_kv * group
    score_scale = 1.0 / math.sqrt(HD)
    blk_rows = min(512, pack_len)
    blocks = pack_len // blk_rows
    places, segment, positions, valid = pack_layout(lengths[0], pack_len)
    first_row = seq_rank * tok_rows
    my_pos = lax.dynamic_slice_in_dim(positions, first_row, tok_rows)
    my_valid = lax.dynamic_slice_in_dim(valid, first_row, tok_rows).astype(jnp.float32)[:, None]
    gain_attn, query_full, key_full, value_full, gain_query, gain_key, out_full = (
        lax.all_gather(attn_gain, "dp", axis=0, tiled=True),
        lax.all_gather(w_query, "dp", axis=0, tiled=True),
        lax.all_gather(w_key, "dp", axis=0, tiled=True),
        lax.all_gather(w_value, "dp", axis=0, tiled=True),
        lax.all_gather(query_gain, "dp", axis=0, tiled=True),
        lax.all_gather(key_gain, "dp", axis=0, tiled=True),
        lax.all_gather(w_out, "dp", axis=0, tiled=True),
    )
    gain_ffn, gate_full, up_full, down_full = (
        lax.all_gather(ffn_gain, "dp", axis=0, tiled=True),
        lax.all_gather(w_gate, "dp", axis=0, tiled=True),
        lax.all_gather(w_up, "dp", axis=0, tiled=True),
        lax.all_gather(w_down, "dp", axis=0, tiled=True),
    )
    normed, pull_attn_norm = jax.vjp(rms_norm, tokens, gain_attn.astype(jnp.float32))
    normed_low = normed.astype(jnp.bfloat16)
    q_lin = jnp.dot(normed_low, query_full, preferred_element_type=jnp.float32)
    k_lin = jnp.dot(normed_low, key_full, preferred_element_type=jnp.float32)
    v_lin = jnp.dot(normed_low, value_full, preferred_element_type=jnp.float32)
    cos_tab, sin_tab = rope_tables(my_pos, HD)
    queries, pull_query = jax.vjp(
        partial(qk_prep, cos_tab=cos_tab, sin_tab=sin_tab, heads=H),
        q_lin,
        gain_query.astype(jnp.float32),
    )
    key_rows, pull_key = jax.vjp(
        partial(qk_prep, cos_tab=cos_tab, sin_tab=sin_tab, heads=KV),
        k_lin,
        gain_key.astype(jnp.float32),
    )
    q_heads, k_heads, v_heads = (
        lax.all_to_all(
            queries.astype(jnp.bfloat16).reshape(tok_rows, seq_count, -1),
            "seq",
            split_axis=1,
            concat_axis=0,
            tiled=True,
        ),
        lax.all_to_all(
            key_rows.astype(jnp.bfloat16).reshape(tok_rows, seq_count, -1),
            "seq",
            split_axis=1,
            concat_axis=0,
            tiled=True,
        ),
        lax.all_to_all(
            v_lin.astype(jnp.bfloat16).reshape(tok_rows, seq_count, -1),
            "seq",
            split_axis=1,
            concat_axis=0,
            tiled=True,
        ),
    )
    query_blocks = q_heads.reshape(blocks, blk_rows, local_kv, group, HD)
    key_all = k_heads.reshape(pack_len, local_kv, HD)
    value_all = v_heads.reshape(pack_len, local_kv, HD)
    seg_blocks = segment.reshape(blocks, blk_rows)
    place_blocks = places.reshape(blocks, blk_rows)

    def scores_of(query_blk, seg_blk, place_blk):
        scores = mat_dot("qkgd,skd->kgqs", query_blk, key_all) * score_scale
        allowed = (seg_blk[:, None] == segment[None, :]) & (places[None, :] <= place_blk[:, None])
        return jnp.where(allowed[None, None], scores, MASKED_SCORE)

    def forward_block(inputs):
        query_blk, seg_blk, place_blk = inputs
        scores = scores_of(query_blk, seg_blk, place_blk)
        top_val = jnp.max(scores, axis=-1, keepdims=True)
        expo = jnp.exp(scores - top_val)
        total = jnp.sum(expo, axis=-1, keepdims=True)
        probs = (expo / total).astype(jnp.bfloat16)
        attended_blk = mat_dot("kgqs,skd->qkgd", probs, value_all)
        return (attended_blk, (top_val + jnp.log(total))[..., 0])

    attended_heads, log_sums = lax.map(forward_block, (query_blocks, seg_blocks, place_blocks))
    attended_send = attended_heads.reshape(pack_len, 1, local_q * HD).astype(jnp.bfloat16)
    attended = lax.all_to_all(
        attended_send, "seq", split_axis=0, concat_axis=1, tiled=True
    ).reshape(tok_rows, -1)
    resid = tokens + jnp.dot(attended, out_full, preferred_element_type=jnp.float32)
    ffn_in, pull_ffn_norm = jax.vjp(rms_norm, resid, gain_ffn.astype(jnp.float32))
    ffn_low = ffn_in.astype(jnp.bfloat16)
    gate_act = jnp.dot(ffn_low, gate_full, preferred_element_type=jnp.float32)
    up_act = jnp.dot(ffn_low, up_full, preferred_element_type=jnp.float32)
    hidden, pull_swiglu = jax.vjp(swiglu, gate_act, up_act)
    hidden_low = hidden.astype(jnp.bfloat16)
    block_out = (
        resid + jnp.dot(hidden_low, down_full, preferred_element_type=jnp.float32)
    ) * my_valid
    query_back, key_back, value_back, out_back = (
        lax.all_gather(w_query, "dp", axis=0, tiled=True),
        lax.all_gather(w_key, "dp", axis=0, tiled=True),
        lax.all_gather(w_value, "dp", axis=0, tiled=True),
        lax.all_gather(w_out, "dp", axis=0, tiled=True),
    )
    gate_back, up_back, down_back = (
        lax.all_gather(w_gate, "dp", axis=0, tiled=True),
        lax.all_gather(w_up, "dp", axis=0, tiled=True),
        lax.all_gather(w_down, "dp", axis=0, tiled=True),
    )
    grad = cotangent * my_valid
    grad_low = grad.astype(jnp.bfloat16)
    d_down = mat_dot("tf,td->fd", hidden_low, grad_low)
    d_hidden = mat_dot("td,fd->tf", grad_low, down_back)
    d_gate, d_up = pull_swiglu(d_hidden)
    d_gate_low = d_gate.astype(jnp.bfloat16)
    d_up_low = d_up.astype(jnp.bfloat16)
    d_gate_w = mat_dot("td,tf->df", ffn_low, d_gate_low)
    d_up_w = mat_dot("td,tf->df", ffn_low, d_up_low)
    d_ffn = mat_dot("tf,df->td", d_gate_low, gate_back) + mat_dot("tf,df->td", d_up_low, up_back)
    d_resid_norm, d_gain_ffn = pull_ffn_norm(d_ffn)
    ffn_shards = (
        lax.psum_scatter(d_gain_ffn, "dp", scatter_dimension=0, tiled=True),
        lax.psum_scatter(d_gate_w, "dp", scatter_dimension=0, tiled=True),
        lax.psum_scatter(d_up_w, "dp", scatter_dimension=0, tiled=True),
        lax.psum_scatter(d_down, "dp", scatter_dimension=0, tiled=True),
    )
    d_resid = grad + d_resid_norm
    resid_low = d_resid.astype(jnp.bfloat16)
    d_out_w = mat_dot("tq,td->qd", attended, resid_low)
    d_attended = mat_dot("td,qd->tq", resid_low, out_back).astype(jnp.bfloat16)
    d_att_heads = lax.all_to_all(
        d_attended.reshape(tok_rows, seq_count, -1), "seq", split_axis=1, concat_axis=0, tiled=True
    )
    d_att_blocks = d_att_heads.reshape(blocks, blk_rows, local_kv, group, HD)

    def backward_block(carry, inputs):
        d_key_acc, d_value_acc = carry
        query_blk, seg_blk, place_blk, log_sum, d_att_blk = inputs
        scores = scores_of(query_blk, seg_blk, place_blk)
        probs = jnp.exp(scores - log_sum[..., None])
        d_value_acc = d_value_acc + mat_dot("kgqs,qkgd->skd", probs.astype(jnp.bfloat16), d_att_blk)
        d_probs = mat_dot("qkgd,skd->kgqs", d_att_blk, value_all)
        delta = jnp.sum(probs * d_probs, axis=-1, keepdims=True)
        d_scores = (probs * (d_probs - delta)).astype(jnp.bfloat16)
        d_query_blk = mat_dot("kgqs,skd->qkgd", d_scores, key_all) * score_scale
        d_key_acc = d_key_acc + mat_dot("kgqs,qkgd->skd", d_scores, query_blk) * score_scale
        return ((d_key_acc, d_value_acc), d_query_blk)

    zero_kv = jnp.zeros((pack_len, local_kv, HD), jnp.float32)
    (d_key_all, d_value_all), d_query_all = lax.scan(
        backward_block,
        (zero_kv, zero_kv),
        (query_blocks, seg_blocks, place_blocks, log_sums, d_att_blocks),
    )
    d_q_tok, d_k_tok, d_v_tok = (
        lax.all_to_all(
            d_query_all.reshape(pack_len, 1, -1).astype(jnp.bfloat16),
            "seq",
            split_axis=0,
            concat_axis=1,
            tiled=True,
        ),
        lax.all_to_all(
            d_key_all.reshape(pack_len, 1, -1).astype(jnp.bfloat16),
            "seq",
            split_axis=0,
            concat_axis=1,
            tiled=True,
        ),
        lax.all_to_all(
            d_value_all.reshape(pack_len, 1, -1).astype(jnp.bfloat16),
            "seq",
            split_axis=0,
            concat_axis=1,
            tiled=True,
        ),
    )
    d_q_lin, d_gain_query = pull_query(d_q_tok.reshape(tok_rows, H, HD).astype(jnp.float32))
    d_k_lin, d_gain_key = pull_key(d_k_tok.reshape(tok_rows, KV, HD).astype(jnp.float32))
    d_q_low = d_q_lin.astype(jnp.bfloat16)
    d_k_low = d_k_lin.astype(jnp.bfloat16)
    d_v_low = d_v_tok.reshape(tok_rows, -1)
    d_query_w = mat_dot("td,tq->dq", normed_low, d_q_low)
    d_key_w = mat_dot("td,tq->dq", normed_low, d_k_low)
    d_value_w = mat_dot("td,tq->dq", normed_low, d_v_low)
    d_normed = (
        mat_dot("tq,dq->td", d_q_low, query_back)
        + mat_dot("tq,dq->td", d_k_low, key_back)
        + mat_dot("tq,dq->td", d_v_low, value_back)
    )
    d_tok_norm, d_gain_attn = pull_attn_norm(d_normed)
    d_tokens = d_resid + d_tok_norm
    attn_shards = (
        lax.psum_scatter(d_gain_attn, "dp", scatter_dimension=0, tiled=True),
        lax.psum_scatter(d_query_w, "dp", scatter_dimension=0, tiled=True),
        lax.psum_scatter(d_key_w, "dp", scatter_dimension=0, tiled=True),
        lax.psum_scatter(d_value_w, "dp", scatter_dimension=0, tiled=True),
        lax.psum_scatter(d_gain_query, "dp", scatter_dimension=0, tiled=True),
        lax.psum_scatter(d_gain_key, "dp", scatter_dimension=0, tiled=True),
        lax.psum_scatter(d_out_w, "dp", scatter_dimension=0, tiled=True),
    )
    summed = lax.psum(
        (
            attn_shards[0],
            attn_shards[1],
            attn_shards[2],
            attn_shards[3],
            attn_shards[4],
            attn_shards[5],
            attn_shards[6],
            ffn_shards[0],
            ffn_shards[1],
            ffn_shards[2],
            ffn_shards[3],
        ),
        "seq",
    )
    return (
        block_out,
        d_tokens,
        summed[0],
        summed[1],
        summed[2],
        summed[3],
        summed[4],
        summed[5],
        summed[6],
        summed[7],
        summed[8],
        summed[9],
        summed[10],
    )


def solution(mesh):
    return jax.shard_map(
        body,
        mesh=mesh,
        in_specs=(
            P(("dp", "seq"), None),
            P("dp", None),
            P("dp"),
            P("dp", None),
            P("dp", None),
            P("dp", None),
            P("dp"),
            P("dp"),
            P("dp", None),
            P("dp"),
            P("dp", None),
            P("dp", None),
            P("dp", None),
            P(("dp", "seq"), None),
        ),
        out_specs=(
            P(("dp", "seq"), None),
            P(("dp", "seq"), None),
            P("dp"),
            P("dp", None),
            P("dp", None),
            P("dp", None),
            P("dp"),
            P("dp"),
            P("dp", None),
            P("dp"),
            P("dp", None),
            P("dp", None),
            P("dp", None),
        ),
        check_vma=False,
    )
```

profile of v0, /device:TPU:0, one launch (start us, length us, event | category | flops | bytes accessed | tf_op | source)
XLA Modules:
  0.0 1586.6 jit_solution(17672986321578510262)
XLA Ops:
  15.5 36.1 %all-reduce.16 = (bf16[64]{0:T(256)(128)(2,1)S(1)}, bf16[1024]{0:T(1024)(128)(2,1)S(1)}, bf16[64]{0:T(256)(128)(2,1)S(1)}, bf16[1024]{0:T(1024)(128)(2,1)}) all-reduce(bf16[64]{0:T(256)(128)(2,1)S(1)} %dynamic-update-slice.1, bf16[1024]{0:T(1024)(128)(2,1)S(1)} %dynamic-update-slice, ...), channel_id=1, replica_groups=mesh['dp'=16,'seq'=2] {'dp'}, use_global_device_ids=true, to_apply=%add.6 | all-reduce | flops 2176 | bytes 8704
  61.4 28.7 %all-gather.12.cloned.1.call-done = bf16[1024,512]{1,0:T(8,128)(2,1)} async-done(((bf16[64,512]{1,0:T(8,128)(2,1)}), bf16[1024,512]{1,0:T(8,128)(2,1)}) %all-gather.12.cloned.1.call-update) | async-done | bytes 1048592 | tf_op jit(solution)/shard_map/all_gather | solution.py:98
  92.9 39.9 %all-gather.8.cloned.1.call-done = bf16[1024,1024]{1,0:T(8,128)(2,1)} async-done(((bf16[64,1024]{1,0:T(8,128)(2,1)}), bf16[1024,1024]{1,0:T(8,128)(2,1)}) %all-gather.8.cloned.1.call-update) | async-done | bytes 2097168 | tf_op jit(solution)/shard_map/all_gather | solution.py:96
  168.3 29.5 %while.28 = (s32[]{:T(128)}, bf16[2,512,4,2,64]{1,4,3,2,0:T(8,128)(2,1)S(1)}, f32[2,4,2,512]{3,2,1,0:T(2,128)S(1)}, s32[2,512]{1,0:T(2,128)S(1)}, s32[2,512]{1,0...) while((s32[]{:T(128)}, ...), condition=%wide.region_7.8_spmd.clone, body=%wide.region_4.7_spmd.clone.sunk | while | flops 1125644288 | bytes 55201920 | solution.py:169
  224.8 12.5 all-to-all-done.3
  267.8 70.4 %all-gather.18.cloned.1.call-done = bf16[1024,4608]{1,0:T(8,128)(2,1)} async-done(((bf16[64,4608]{1,0:T(8,128)(2,1)}), bf16[1024,4608]{1,0:T(8,128)(2,1)}) %all-gather.18.cloned.1.call-update) | async-done | bytes 9437200 | tf_op jit(solution)/shard_map/all_gather | solution.py:106
  349.4 70.5 %all-gather.20.cloned.1.call-done = bf16[4608,1024]{1,0:T(8,128)(2,1)} async-done(((bf16[288,1024]{1,0:T(8,128)(2,1)}), bf16[4608,1024]{1,0:T(8,128)(2,1)}) %all-gather.20.cloned.1.call-update) | async-done | bytes 9437200 | tf_op jit(solution)/shard_map/all_gather | solution.py:107
  419.9 18.5 %multiply_convert_fusion = (bf16[512,4608]{1,0:T(8,128)(2,1)}, bf16[512,4608]{1,0:T(8,128)(2,1)}, bf16[512,4608]{1,0:T(8,128)(2,1)}) fusion(f32[512,4608]{1,0:T(8,128)} %fusion.78, f32[512,4608]{1,0:T(8,128)} %fusion.79, bf16[4608,1024]{1,0:T(8,128)(2,1)} %all-gather.20.cloned.1.call-done, f32[512,1024]{1,0:T(8,128)} %param.31, ...), kind=kOutput, calls=%fused_computation.73 | convolution fusion | flops 4870635520 | bytes 44566528 | tf_op jit(solution)/shard_map/td,fd->tf/dot_general | solution.py:61
  464.4 14.2 all-to-all-done.4
  481.0 87.6 %while.29 = (s32[]{:T(128)}, f32[1024,4,64]{0,2,1:T(8,128)}, f32[1024,4,64]{0,2,1:T(8,128)}, bf16[2,512,4,2,64]{1,4,3,2,0:T(8,128)(2,1)}, bf16[2,512,4,2,64]{1,4...) while((s32[]{:T(128)}, f32[1024,4,64]{0,2,1:T(8,128)}, ...), condition=%wide.region_12.13_spmd.clone, body=%wide.region_10.12_spmd.clone.sunk | while | flops 2725246976 | bytes 186356192 | solution.py:235
  486.5 11.2 fusion.165
  530.3 11.2 fusion.165
  631.7 15.2 all_to_all.110
  661.4 11.6 fusion.86
  673.1 11.5 fusion.87
  686.2 11.6 fusion.75
  698.1 14.7 reduce-scatter.12.cloned.1.call-done
  712.8 75.4 %reduce-scatter.14.cloned.1.call-done = f32[64,1024]{1,0:T(8,128)} async-done(((f32[1024,1024]{1,0:T(8,128)}), f32[64,1024]{1,0:T(8,128)}) %reduce-scatter.14.cloned.1.call-update) | async-done | bytes 262160 | tf_op jit(solution)/shard_map/reduce_scatter | solution.py:285
  788.2 75.7 %reduce-scatter.8.cloned.1.call-done = f32[64,1024]{1,0:T(8,128)} async-done(((f32[1024,1024]{1,0:T(8,128)}), f32[64,1024]{1,0:T(8,128)}) %reduce-scatter.8.cloned.1.call-update) | async-done | bytes 262160 | tf_op jit(solution)/shard_map/reduce_scatter | solution.py:280
  864.0 197.1 %reduce-scatter.16.cloned.1.call-done = f32[64,4608]{1,0:T(8,128)} async-done(((f32[1024,4608]{1,0:T(8,128)}), f32[64,4608]{1,0:T(8,128)}) %reduce-scatter.16.cloned.1.call-update) | async-done | bytes 1179664 | tf_op jit(solution)/shard_map/reduce_scatter | solution.py:208
  1061.1 197.3 %reduce-scatter.18.cloned.1.call-done = f32[64,4608]{1,0:T(8,128)} async-done(((f32[1024,4608]{1,0:T(8,128)}), f32[64,4608]{1,0:T(8,128)}) %reduce-scatter.18.cloned.1.call-update) | async-done | bytes 1179664 | tf_op jit(solution)/shard_map/reduce_scatter | solution.py:209
  1258.4 197.1 %reduce-scatter.20.cloned.1.call-done = f32[288,1024]{1,0:T(8,128)} async-done(((f32[4608,1024]{1,0:T(8,128)}), f32[288,1024]{1,0:T(8,128)}) %reduce-scatter.20.cloned.1.call-update) | async-done | bytes 1179664 | tf_op jit(solution)/shard_map/reduce_scatter | solution.py:210
  1473.6 32.5 %all-reduce.13 = (f32[1024]{0:T(1024)S(1)}, f32[64]{0:T(128)S(1)}, f32[64]{0:T(128)S(1)}, f32[1024]{0:T(1024)S(1)}) all-reduce(f32[1024]{0:T(1024)S(1)} %get-tuple-element.220, f32[64]{0:T(128)S(1)} %get-tuple-element.222, f32[64]{0:T(128)S(1)} %get-tuple-element.224, ...), channel_id=2, replica_groups=mesh['dp'=16,'seq'=2] {'dp'}, use_global_device_ids=true, to_apply=%region_17.18.clone | all-reduce | flops 2176 | bytes 17408
  1516.0 52.5 %all-reduce.19.cloned.1.call-done = (f32[64,1024]{1,0:T(8,128)}, f32[64,512]{1,0:T(8,128)}, f32[64,512]{1,0:T(8,128)}, f32[64,1024]{1,0:T(8,128)}, f32[64,4608]{...) async-done(((f32[64,1024]{1,0:T(8,128)}, f32[64,512]{1,0:T(8,128)}, f32[64,512]{1,0:T(8,128)}, f32[64,1024]{1,0:T(8,128)}, f32[64,4608]{1,0:T(8,128)}, ...) | async-done | bytes 4325392 | tf_op jit(solution)/shard_map/psum | solution.py:287
  (365 shorter events, 362.0 us)
Async XLA Ops:
  7.2 46.0 %all-gather.10.cloned.1.call-start = ((), (), s32[]{:S(2)}) async-start(), calls=%async_computation.16 | async-start | bytes 1114112 | tf_op jit(solution)/shard_map/all_gather | solution.py:97
  8.0 82.2 %all-gather.12.cloned.1.call-start = ((), (), s32[]{:S(2)}) async-start(), calls=%async_computation.17 | async-start | bytes 1114112 | tf_op jit(solution)/shard_map/all_gather | solution.py:98
  8.7 124.0 %all-gather.8.cloned.1.call-start = ((), (), s32[]{:S(2)}) async-start(), calls=%async_computation.15 | async-start | bytes 2228224 | tf_op jit(solution)/shard_map/all_gather | solution.py:96
  9.5 235.5 %all-gather.14.cloned.1.call-start = ((), (), s32[]{:S(2)}) async-start(), calls=%async_computation.18 | async-start | bytes 2228224 | tf_op jit(solution)/shard_map/all_gather | solution.py:101
  10.0 246.7 %all-gather.16.cloned.1.call-start = ((), (), s32[]{:S(2)}) async-start(), calls=%async_computation.19 | async-start | bytes 10027008 | tf_op jit(solution)/shard_map/all_gather | solution.py:105
  10.6 327.6 %all-gather.18.cloned.1.call-start = ((), (), s32[]{:S(2)}) async-start(), calls=%async_computation.20 | async-start | bytes 10027008 | tf_op jit(solution)/shard_map/all_gather | solution.py:106
  11.2 408.7 %all-gather.20.cloned.1.call-start = ((), (), s32[]{:S(2)}) async-start(), calls=%async_computation.21 | async-start | bytes 10027008 | tf_op jit(solution)/shard_map/all_gather | solution.py:107
  53.2 87.8 %copy-start.31 = (f32[512,32]{0,1:T(8,128)}, f32[512,32]{0,1:T(8,128)S(1)}, u32[]{:S(2)}) copy-start(f32[512,32]{0,1:T(8,128)S(1)} %get-tuple-element.306) | copy-start | bytes 196612
  53.2 87.8 %copy-start.33 = (f32[512,32]{0,1:T(8,128)}, f32[512,32]{0,1:T(8,128)S(1)}, u32[]{:S(2)}) copy-start(f32[512,32]{0,1:T(8,128)S(1)} %get-tuple-element.307) | copy-start | bytes 196612
  57.2 80.3 %all-to-all-start.1 = ((bf16[512,2,256]{0,2,1:T(8,128)(2,1)}), bf16[512,2,256]{0,2,1:T(8,128)(2,1)}, u32[]{:S(2)}, u32[]{:S(2)}) async-start(bf16[512,2,256]{0,2,1:T(8,128)(2,1)} %bitcast.10), calls=%async_computation.1 | async-start | bytes 1048576 | tf_op jit(solution)/shard_map/all_to_all | solution.py:133
  137.5 12.1 all-to-all-start.2
  149.6 18.5 %all-to-all-start = ((bf16[512,2,512]{0,2,1:T(8,128)(2,1)}), bf16[512,2,512]{0,2,1:T(8,128)(2,1)}, u32[]{:S(2)}, u32[]{:S(2)}) async-start(bf16[512,2,512]{0,2,1:T(8,128)(2,1)} %bitcast.5), calls=%async_computation | async-start | bytes 2097152 | tf_op jit(solution)/shard_map/all_to_all | solution.py:126
  221.1 16.2 %all-to-all-start.3 = ((bf16[2,2,131072]{2,1,0:T(2,128)(2,1)}), bf16[2,2,131072]{2,1,0:T(2,128)(2,1)S(1)}, u32[]{:S(2)}, u32[]{:S(2)}) async-start(bf16[2,2,131072]{2,1,0:T(2,128)(2,1)} %reshape.492), calls=%async_computation.3 | async-start | bytes 2097152 | tf_op jit(solution)/shard_map/all_to_all | solution.py:171
  224.8 232.0 %copy-start.57 = (f32[512]{0:T(512)}, f32[512]{0:T(512)S(1)}, u32[]{:S(2)}) copy-start(f32[512]{0:T(512)S(1)} %dynamic-slice_convert_fusion.1) | copy-start | bytes 6148
  249.8 88.5 %copy-start.17 = (bf16[512,1024]{1,0:T(8,128)(2,1)}, bf16[512,1024]{1,0:T(8,128)(2,1)S(1)}, u32[]{:S(2)}) copy-start(bf16[512,1024]{1,0:T(8,128)(2,1)S(1)} %multiply_convert_fusion.2) | copy-start | bytes 3145732
  460.8 17.9 %all-to-all-start.4 = ((bf16[512,2,512]{2,0,1:T(8,128)(2,1)}), bf16[512,2,512]{2,0,1:T(8,128)(2,1)S(1)}, u32[]{:S(2)}, u32[]{:S(2)}) async-start(bf16[512,2,512]{2,0,1:T(8,128)(2,1)} %bitcast.213), calls=%async_computation.4 | async-start | bytes 2097152 | tf_op jit(solution)/shard_map/all_to_all | solution.py:216
  464.4 233.8 %reduce-scatter.10.cloned.1.call-start = ((), (), s32[]{:S(2)}) async-start(), calls=%async_computation.23 | async-start | bytes 2228224 | tf_op jit(solution)/shard_map/reduce_scatter | solution.py:281
  588.8 124.1 %reduce-scatter.12.cloned.1.call-start = ((), (), s32[]{:S(2)}) async-start(), calls=%async_computation.24 | async-start | bytes 2228224 | tf_op jit(solution)/shard_map/reduce_scatter | solution.py:282
  604.6 183.7 %reduce-scatter.14.cloned.1.call-start = ((), (), s32[]{:S(2)}) async-start(), calls=%async_computation.25 | async-start | bytes 4456448 | tf_op jit(solution)/shard_map/reduce_scatter | solution.py:285
  609.2 254.8 %reduce-scatter.8.cloned.1.call-start = ((), (), s32[]{:S(2)}) async-start(), calls=%async_computation.22 | async-start | bytes 4456448 | tf_op jit(solution)/shard_map/reduce_scatter | solution.py:280
  660.2 400.9 %reduce-scatter.16.cloned.1.call-start = ((), (), s32[]{:S(2)}) async-start(), calls=%async_computation.26 | async-start | bytes 20054016 | tf_op jit(solution)/shard_map/reduce_scatter | solution.py:208
  673.0 585.4 %reduce-scatter.18.cloned.1.call-start = ((), (), s32[]{:S(2)}) async-start(), calls=%async_computation.27 | async-start | bytes 20054016 | tf_op jit(solution)/shard_map/reduce_scatter | solution.py:209
  684.6 770.9 %reduce-scatter.20.cloned.1.call-start = ((), (), s32[]{:S(2)}) async-start(), calls=%async_computation.28 | async-start | bytes 20054016 | tf_op jit(solution)/shard_map/reduce_scatter | solution.py:210
  697.8 870.7 %all-reduce.19.cloned.1.call-start = ((), (), s32[]{:S(2)}) async-start(), calls=%async_computation.29 | async-start | bytes 8650752 | tf_op jit(solution)/shard_map/psum | solution.py:287
  (80 other events, 538.7 us)
Sparse Core Ops, SparseCore 0:
  10.2 40.6 all-gather.9
  53.1 36.9 all-gather.11
  92.3 40.4 all-gather.7
  134.8 40.1 all-gather.13
  177.1 79.6 all-gather.15
  258.9 79.3 all-gather.17
  340.5 79.3 all-gather.19
  588.9 59.4 reduce-scatter.9
  652.1 60.7 reduce-scatter.11
  716.5 71.6 reduce-scatter.13
  792.1 71.8 reduce-scatter.7
  867.9 193.1 reduce-scatter.15
  1065.2 193.1 reduce-scatter.17
  1262.3 193.0 reduce-scatter.19
  1458.4 110.0 all-reduce.18
where the time goes:
time: 1590 us
  waiting for transfers between devices  1080 us (68%)
  matrix products  215 us (14%)
  blocking collectives  109 us (7%)
  local copies, waits for them, and re-layouts  80.8 us (5%)
  other arithmetic  66.4 us (4%)
  starting transfers between devices  20.7 us (1%)
  between operations  18.9 us (1%)
    reduce_scatter x1, waiting for transfers between devices, body(): lax.psum_scatter(d_up_w, 'dp', scatter_dimension=0, tiled=True)  197 us
    reduce_scatter x1, waiting for transfers between devices, body(): lax.psum_scatter(d_gate_w, 'dp', scatter_dimension=0, tiled=True)  197 us
    reduce_scatter x1, waiting for transfers between devices, body(): lax.psum_scatter(d_down, 'dp', scatter_dimension=0, tiled=True)  197 us
    dot_general x28, matrix products, mat_dot(): return jnp.einsum(form, left, right, preferred_element_type=jnp.float32)  172 us
    reduce_scatter x1, waiting for transfers between devices, body(): lax.psum_scatter(d_query_w, 'dp', scatter_dimension=0, tiled=True)  75.7 us
    reduce_scatter x1, waiting for transfers between devices, body(): lax.psum_scatter(d_out_w, 'dp', scatter_dimension=0, tiled=True)  75.4 us
    all_gather x1, waiting for transfers between devices, body(): lax.all_gather(w_down, 'dp', axis=0, tiled=True)  70.5 us
    all_gather x1, waiting for transfers between devices, body(): lax.all_gather(w_up, 'dp', axis=0, tiled=True)  70.4 us
  transfers between devices with their start and end apart: 20, of which 16 were waited for; matrix products, arithmetic and copies ran while one was open for 13% of the time, Pallas kernels for 0%

commit v1 on v0

--- a/solution.py
+++ b/solution.py
@@ -11,6 +11,19 @@
 EPSILON = 1e-05
 ROPE_BASE = 1000000.0
 MASKED_SCORE = -1e30
+
+
+def collect(value, axis, dim):
+    ways = lax.axis_size(axis)
+    up = [(d, (d + 1) % ways) for d in range(ways)]
+    down = [(d, (d - 1) % ways) for d in range(ways)]
+    earlier, later = ([value], [value])
+    for _ in range(ways // 2):
+        earlier.append(lax.ppermute(earlier[-1], axis, up))
+    for _ in range((ways - 1) // 2):
+        later.append(lax.ppermute(later[-1], axis, down))
+    line = jnp.concatenate([*earlier[::-1], *later[1:]], axis=dim)
+    return jnp.roll(line, (lax.axis_index(axis) - ways // 2) * value.shape[dim], axis=dim)
 
 
 def rms_norm(values, gain_vec):
@@ -103,7 +116,7 @@
     gain_ffn, gate_full, up_full, down_full = (
         lax.all_gather(ffn_gain, "dp", axis=0, tiled=True),
         lax.all_gather(w_gate, "dp", axis=0, tiled=True),
-        lax.all_gather(w_up, "dp", axis=0, tiled=True),
+        collect(w_up, "dp", 0),
         lax.all_gather(w_down, "dp", axis=0, tiled=True),
     )
     normed, pull_attn_norm = jax.vjp(rms_norm, tokens, gain_attn.astype(jnp.float32))

time: 1590 us -> 1630 us (1.025)
  waiting for transfers between devices: 1080 us -> 977 us
  local copies, waits for them, and re-layouts: 80.8 us -> 148 us
  starting transfers between devices: 20.7 us -> 72.3 us
    ppermute x0 -> x15, starting transfers between devices: none -> 52.1 us  [the longest x8 34.3 us: collect(): earlier.append(lax.ppermute(earlier[-1], axis, up))]
    unnamed x160 -> x203, local copies, waits for them, and re-layouts: 40.8 us -> 90.9 us
    all_gather x1, waiting for transfers between devices: 28.7 us -> 0.02 us  [body(): lax.all_gather(w_value, 'dp', axis=0, tiled=True)]
    all_gather x1, waiting for transfers between devices: 70.4 us -> 43 us  [body(): lax.all_gather(w_up, 'dp', axis=0, tiled=True)]
    ppermute x0 -> x15, waiting for transfers between devices: none -> 27.2 us  [the longest x8 18 us: collect(): earlier.append(lax.ppermute(earlier[-1], axis, up))]
    all_gather x1, waiting for transfers between devices: 39.9 us -> 17 us  [body(): lax.all_gather(w_query, 'dp', axis=0, tiled=True)]
    all_gather x1, waiting for transfers between devices: 70.5 us -> 51.8 us  [body(): lax.all_gather(w_down, 'dp', axis=0, tiled=True)]
  transfers between devices with their start and end apart: 20 -> 35, of which waited for: 16 -> 19; matrix products, arithmetic and copies ran while one was open for 13% -> 18% of each run, Pallas kernels for 0% -> 0%
where the time goes in v1:
time: 1630 us; the launch traced here: 1620 us
  waiting for transfers between devices  977 us (60%)
  matrix products  226 us (14%)
  local copies, waits for them, and re-layouts  148 us (9%)
  blocking collectives  107 us (7%)
  other arithmetic  72.9 us (4%)
  starting transfers between devices  72.3 us (4%)
  between operations  18.9 us (1%)
    reduce_scatter x1, waiting for transfers between devices, body(): lax.psum_scatter(d_up_w, 'dp', scatter_dimension=0, tiled=True)  197 us
    reduce_scatter x1, waiting for transfers between devices, body(): lax.psum_scatter(d_down, 'dp', scatter_dimension=0, tiled=True)  197 us
    reduce_scatter x1, waiting for transfers between devices, body(): lax.psum_scatter(d_gate_w, 'dp', scatter_dimension=0, tiled=True)  197 us
    dot_general x28, matrix products, mat_dot(): return jnp.einsum(form, left, right, preferred_element_type=jnp.float32)  176 us
    unnamed x203, local copies, waits for them, and re-layouts  90.9 us
    reduce_scatter x1, waiting for transfers between devices, body(): lax.psum_scatter(d_query_w, 'dp', scatter_dimension=0, tiled=True)  75.7 us
    reduce_scatter x1, waiting for transfers between devices, body(): lax.psum_scatter(d_out_w, 'dp', scatter_dimension=0, tiled=True)  75.5 us
    unnamed x2, blocking collectives  65.1 us
  transfers between devices with their start and end apart: 35, of which 19 were waited for; matrix products, arithmetic and copies ran while one was open for 18% of the time, Pallas kernels for 0%

profile of v1, /device:TPU:0, one launch (start us, length us, event | category | flops | bytes accessed | tf_op | source)
XLA Modules:
  0.0 1622.2 jit_solution(11033153958591615327)
XLA Ops:
  52.8 32.6 %all-reduce.16 = (bf16[64]{0:T(256)(128)(2,1)S(1)}, bf16[1024]{0:T(1024)(128)(2,1)S(1)}, bf16[64]{0:T(256)(128)(2,1)S(1)}, bf16[1024]{0:T(1024)(128)(2,1)S(1)}) all-reduce(bf16[64]{0:T(256)(128)(2,1)S(1)} %dynamic-update-slice.1, bf16[1024]{0:T(1024)(128)(2,1)S(1)} %dynamic-update-slice, ...), channel_id=1, replica_groups=mesh['dp'=16,'seq'=2] {'dp'}, use_global_device_ids=true, to_apply=%add.6 | all-reduce | flops 2176 | bytes 8704
  142.8 17.0 %all-gather.8.cloned.1.call-done = bf16[1024,1024]{1,0:T(8,128)(2,1)} async-done(((bf16[64,1024]{1,0:T(8,128)(2,1)}), bf16[1024,1024]{1,0:T(8,128)(2,1)}) %all-gather.8.cloned.1.call-update) | async-done | bytes 2097168 | tf_op jit(solution)/shard_map/all_gather | solution.py:109
  193.9 27.2 %while.28 = (s32[]{:T(128)}, bf16[2,512,4,2,64]{1,4,3,2,0:T(8,128)(2,1)S(1)}, f32[2,4,2,512]{3,2,1,0:T(2,128)S(1)}, s32[2,512]{1,0:T(2,128)S(1)}, s32[2,512]{1,0...) while((s32[]{:T(128)}, ...), condition=%wide.region_7.8_spmd.clone, body=%wide.region_4.7_spmd.clone.sunk | while | flops 1125644288 | bytes 55201912 | solution.py:182
  310.4 11.4 fusion.81
  321.8 51.8 %all-gather.18.cloned.1.call-done = bf16[4608,1024]{1,0:T(8,128)(2,1)} async-done(((bf16[288,1024]{1,0:T(8,128)(2,1)}), bf16[4608,1024]{1,0:T(8,128)(2,1)}) %all-gather.18.cloned.1.call-update) | async-done | bytes 9437200 | tf_op jit(solution)/shard_map/all_gather | solution.py:120
  373.6 11.7 fusion.79
  385.3 16.9 %multiply_convert_fusion = (bf16[512,4608]{1,0:T(8,128)(2,1)}, bf16[512,4608]{1,0:T(8,128)(2,1)}, bf16[512,4608]{1,0:T(8,128)(2,1)}) fusion(f32[512,4608]{1,0:T(8,128)} %fusion.79, f32[512,4608]{1,0:T(8,128)} %fusion.81, bf16[512,1024]{1,0:T(8,128)(2,1)S(1)} %multiply_convert_fusion.2, bf16[2048,4608]{1,0:T(8,128)(2,1)} %constant_dynamic-update-slice_fusion, ...), kind=kOutput, calls=%fused_computation.73 | convolution fusion | flops 4869586944 | bytes 43515908 | tf_op jit(solution)/shard_map/dot_general | solution.py:191
  412.3 43.0 %all-gather.20.cloned.1.call-done = bf16[1024,4608]{1,0:T(8,128)(2,1)} async-done(((bf16[64,4608]{1,0:T(8,128)(2,1)}), bf16[1024,4608]{1,0:T(8,128)(2,1)}) %all-gather.20.cloned.1.call-update) | async-done | bytes 9437200 | tf_op jit(solution)/shard_map/all_gather | solution.py:205
  455.3 11.2 multiply_reduce_fusion
  475.3 14.3 all-to-all-done.4
  492.2 109.8 %while.29 = (s32[]{:T(128)}, f32[1024,4,64]{0,2,1:T(8,128)}, f32[1024,4,64]{0,2,1:T(8,128)}, bf16[2,512,4,2,64]{1,4,3,2,0:T(8,128)(2,1)}, bf16[2,512,4,2,64]{1,4...) while((s32[]{:T(128)}, f32[1024,4,64]{0,2,1:T(8,128)}, ...), condition=%wide.region_12.13_spmd.clone, body=%wide.region_10.12_spmd.clone.sunk | while | flops 2725246976 | bytes 286889792 | solution.py:248
  558.2 10.1 fusion.166
  604.8 10.7 all_to_all.108
  673.1 15.2 all_to_all.110
  703.3 11.8 fusion.88
  715.1 11.6 fusion.89
  728.4 11.5 fusion.78
  748.5 75.5 %reduce-scatter.14.cloned.1.call-done = f32[64,1024]{1,0:T(8,128)} async-done(((f32[1024,1024]{1,0:T(8,128)}), f32[64,1024]{1,0:T(8,128)}) %reduce-scatter.14.cloned.1.call-update) | async-done | bytes 262160 | tf_op jit(solution)/shard_map/reduce_scatter | solution.py:298
  824.0 75.7 %reduce-scatter.8.cloned.1.call-done = f32[64,1024]{1,0:T(8,128)} async-done(((f32[1024,1024]{1,0:T(8,128)}), f32[64,1024]{1,0:T(8,128)}) %reduce-scatter.8.cloned.1.call-update) | async-done | bytes 262160 | tf_op jit(solution)/shard_map/reduce_scatter | solution.py:293
  899.7 197.1 %reduce-scatter.16.cloned.1.call-done = f32[64,4608]{1,0:T(8,128)} async-done(((f32[1024,4608]{1,0:T(8,128)}), f32[64,4608]{1,0:T(8,128)}) %reduce-scatter.16.cloned.1.call-update) | async-done | bytes 1179664 | tf_op jit(solution)/shard_map/reduce_scatter | solution.py:221
  1096.8 197.3 %reduce-scatter.18.cloned.1.call-done = f32[64,4608]{1,0:T(8,128)} async-done(((f32[1024,4608]{1,0:T(8,128)}), f32[64,4608]{1,0:T(8,128)}) %reduce-scatter.18.cloned.1.call-update) | async-done | bytes 1179664 | tf_op jit(solution)/shard_map/reduce_scatter | solution.py:222
  1294.0 197.1 %reduce-scatter.20.cloned.1.call-done = f32[288,1024]{1,0:T(8,128)} async-done(((f32[4608,1024]{1,0:T(8,128)}), f32[288,1024]{1,0:T(8,128)}) %reduce-scatter.20.cloned.1.call-update) | async-done | bytes 1179664 | tf_op jit(solution)/shard_map/reduce_scatter | solution.py:223
  1507.9 32.5 %all-reduce.13 = (f32[1024]{0:T(1024)S(1)}, f32[64]{0:T(128)S(1)}, f32[64]{0:T(128)S(1)}, f32[1024]{0:T(1024)S(1)}) all-reduce(f32[1024]{0:T(1024)S(1)} %get-tuple-element.220, f32[64]{0:T(128)S(1)} %get-tuple-element.222, f32[64]{0:T(128)S(1)} %get-tuple-element.224, ...), channel_id=2, replica_groups=mesh['dp'=16,'seq'=2] {'dp'}, use_global_device_ids=true, to_apply=%region_17.18.clone | all-reduce | flops 2176 | bytes 17408
  1550.4 53.8 %all-reduce.19.cloned.1.call-done = (f32[64,1024]{1,0:T(8,128)}, f32[64,512]{1,0:T(8,128)}, f32[64,512]{1,0:T(8,128)}, f32[64,1024]{1,0:T(8,128)}, f32[64,4608]{...) async-done(((f32[64,1024]{1,0:T(8,128)}, f32[64,512]{1,0:T(8,128)}, f32[64,512]{1,0:T(8,128)}, f32[64,1024]{1,0:T(8,128)}, f32[64,4608]{1,0:T(8,128)}, ...) | async-done | bytes 4325392 | tf_op jit(solution)/shard_map/psum | solution.py:300
  (421 shorter events, 493.4 us)
Async XLA Ops:
  7.2 98.9 %all-gather.10.cloned.1.call-start = ((), (), s32[]{:S(2)}) async-start(), calls=%async_computation.16 | async-start | bytes 1114112 | tf_op jit(solution)/shard_map/all_gather | solution.py:110
  7.9 120.6 %all-gather.12.cloned.1.call-start = ((), (), s32[]{:S(2)}) async-start(), calls=%async_computation.17 | async-start | bytes 1114112 | tf_op jit(solution)/shard_map/all_gather | solution.py:111
  8.7 151.2 %all-gather.8.cloned.1.call-start = ((), (), s32[]{:S(2)}) async-start(), calls=%async_computation.15 | async-start | bytes 2228224 | tf_op jit(solution)/shard_map/all_gather | solution.py:109
  9.4 295.4 %all-gather.14.cloned.1.call-start = ((), (), s32[]{:S(2)}) async-start(), calls=%async_computation.18 | async-start | bytes 2228224 | tf_op jit(solution)/shard_map/all_gather | solution.py:114
  10.0 300.4 %all-gather.16.cloned.1.call-start = ((), (), s32[]{:S(2)}) async-start(), calls=%async_computation.19 | async-start | bytes 10027008 | tf_op jit(solution)/shard_map/all_gather | solution.py:118
  10.6 363.0 %all-gather.18.cloned.1.call-start = ((), (), s32[]{:S(2)}) async-start(), calls=%async_computation.20 | async-start | bytes 10027008 | tf_op jit(solution)/shard_map/all_gather | solution.py:120
  29.3 58.1 %collective-permute-start.9 = (bf16[64,4608]{1,0:T(8,128)(2,1)S(1)}, bf16[64,4608]{1,0:T(8,128)(2,1)}, u32[]{:S(2)}, u32[]{:S(2)}) collective-permute-start(bf16[64,4608]{1,0:T(8,128)(2,1)S(1)} %collective-permute-done.8), channel_id=1, source_target_pairs={{0,30},{2,0},{4,2},{6,4},{8,6},{10,8},{12,10},{14,12},{16,14},{18,... | collective-permute-start | bytes 1769480 | tf_op jit(solution)/shard_map/ppermute | solution.py:24
  37.6 49.9 %collective-permute-start.2 = (bf16[64,4608]{1,0:T(8,128)(2,1)S(1)}, bf16[64,4608]{1,0:T(8,128)(2,1)}, u32[]{:S(2)}, u32[]{:S(2)}) collective-permute-start(bf16[64,4608]{1,0:T(8,128)(2,1)S(1)} %collective-permute-done.1), channel_id=1, source_target_pairs={{0,2},{2,4},{4,6},{6,8},{8,10},{10,12},{12,14},{14,16},{16,18},{18... | collective-permute-start | bytes 1769480 | tf_op jit(solution)/shard_map/ppermute | solution.py:22
  109.8 21.6 %collective-permute-start.12 = (bf16[64,4608]{1,0:T(8,128)(2,1)S(1)}, bf16[64,4608]{1,0:T(8,128)(2,1)}, u32[]{:S(2)}, u32[]{:S(2)}) collective-permute-start(bf16[64,4608]{1,0:T(8,128)(2,1)S(1)} %collective-permute-done.11), channel_id=1, source_target_pairs={{0,30},{2,0},{4,2},{6,4},{8,6},{10,8},{12,10},{14,12},{16,14},{18,... | collective-permute-start | bytes 1769480 | tf_op jit(solution)/shard_map/ppermute | solution.py:24
  124.3 40.3 %all-to-all-start.1 = ((bf16[512,2,256]{0,2,1:T(8,128)(2,1)}), bf16[512,2,256]{0,2,1:T(8,128)(2,1)}, u32[]{:S(2)}, u32[]{:S(2)}) async-start(bf16[512,2,256]{0,2,1:T(8,128)(2,1)} %bitcast.10), calls=%async_computation.1 | async-start | bytes 1048576 | tf_op jit(solution)/shard_map/all_to_all | solution.py:146
  131.3 53.9 %collective-permute-start.13 = (bf16[64,4608]{1,0:T(8,128)(2,1)}, bf16[64,4608]{1,0:T(8,128)(2,1)}, u32[]{:S(2)}, u32[]{:S(2)}) collective-permute-start(bf16[64,4608]{1,0:T(8,128)(2,1)} %collective-permute-done.12), channel_id=1, source_target_pairs={{0,30},{2,0},{4,2},{6,4},{8,6},{10,8},{12,10},{14,12},{16,14},{18,... | collective-permute-start | bytes 1769480 | tf_op jit(solution)/shard_map/ppermute | solution.py:24
  134.3 51.8 %collective-permute-start.6 = (bf16[64,4608]{1,0:T(8,128)(2,1)}, bf16[64,4608]{1,0:T(8,128)(2,1)}, u32[]{:S(2)}, u32[]{:S(2)}) collective-permute-start(bf16[64,4608]{1,0:T(8,128)(2,1)} %collective-permute-done.5), channel_id=1, source_target_pairs={{0,2},{2,4},{4,6},{6,8},{8,10},{10,12},{12,14},{14,16},{16,18},{18... | collective-permute-start | bytes 1769480 | tf_op jit(solution)/shard_map/ppermute | solution.py:22
  180.3 274.9 %all-gather.20.cloned.1.call-start = ((), (), s32[]{:S(2)}) async-start(), calls=%async_computation.21 | async-start | bytes 10027008 | tf_op jit(solution)/shard_map/all_gather | solution.py:205
  185.3 86.6 %collective-permute-start.14 = (bf16[64,4608]{1,0:T(8,128)(2,1)}, bf16[64,4608]{1,0:T(8,128)(2,1)}, u32[]{:S(2)}, u32[]{:S(2)}) collective-permute-start(bf16[64,4608]{1,0:T(8,128)(2,1)} %collective-permute-done.13), channel_id=1, source_target_pairs={{0,30},{2,0},{4,2},{6,4},{8,6},{10,8},{12,10},{14,12},{16,14},{18,... | collective-permute-start | bytes 1769480 | tf_op jit(solution)/shard_map/ppermute | solution.py:24
  186.1 61.7 %collective-permute-start.7 = (bf16[64,4608]{1,0:T(8,128)(2,1)}, bf16[64,4608]{1,0:T(8,128)(2,1)}, u32[]{:S(2)}, u32[]{:S(2)}) collective-permute-start(bf16[64,4608]{1,0:T(8,128)(2,1)} %collective-permute-done.6), channel_id=1, source_target_pairs={{0,2},{2,4},{4,6},{6,8},{8,10},{10,12},{12,14},{14,16},{16,18},{18... | collective-permute-start | bytes 1769480 | tf_op jit(solution)/shard_map/ppermute | solution.py:22
  244.1 54.2 %all-to-all-start.3 = ((bf16[2,2,131072]{2,1,0:T(2,128)(2,1)}), bf16[2,2,131072]{2,1,0:T(2,128)(2,1)S(1)}, u32[]{:S(2)}, u32[]{:S(2)}) async-start(bf16[2,2,131072]{2,1,0:T(2,128)(2,1)} %reshape.492), calls=%async_computation.3 | async-start | bytes 2097152 | tf_op jit(solution)/shard_map/all_to_all | solution.py:184
  475.3 264.9 %reduce-scatter.10.cloned.1.call-start = ((), (), s32[]{:S(2)}) async-start(), calls=%async_computation.23 | async-start | bytes 2228224 | tf_op jit(solution)/shard_map/reduce_scatter | solution.py:294
  624.5 124.0 %reduce-scatter.12.cloned.1.call-start = ((), (), s32[]{:S(2)}) async-start(), calls=%async_computation.24 | async-start | bytes 2228224 | tf_op jit(solution)/shard_map/reduce_scatter | solution.py:295
  646.0 178.0 %reduce-scatter.14.cloned.1.call-start = ((), (), s32[]{:S(2)}) async-start(), calls=%async_computation.25 | async-start | bytes 4456448 | tf_op jit(solution)/shard_map/reduce_scatter | solution.py:298
  650.6 249.1 %reduce-scatter.8.cloned.1.call-start = ((), (), s32[]{:S(2)}) async-start(), calls=%async_computation.22 | async-start | bytes 4456448 | tf_op jit(solution)/shard_map/reduce_scatter | solution.py:293
  703.2 393.6 %reduce-scatter.16.cloned.1.call-start = ((), (), s32[]{:S(2)}) async-start(), calls=%async_computation.26 | async-start | bytes 20054016 | tf_op jit(solution)/shard_map/reduce_scatter | solution.py:221
  715.1 578.9 %reduce-scatter.18.cloned.1.call-start = ((), (), s32[]{:S(2)}) async-start(), calls=%async_computation.27 | async-start | bytes 20054016 | tf_op jit(solution)/shard_map/reduce_scatter | solution.py:222
  726.8 764.4 %reduce-scatter.20.cloned.1.call-start = ((), (), s32[]{:S(2)}) async-start(), calls=%async_computation.28 | async-start | bytes 20054016 | tf_op jit(solution)/shard_map/reduce_scatter | solution.py:223
  739.8 864.3 %all-reduce.19.cloned.1.call-start = ((), (), s32[]{:S(2)}) async-start(), calls=%async_computation.29 | async-start | bytes 8650752 | tf_op jit(solution)/shard_map/psum | solution.py:300
  (93 other events, 2315.0 us)
Sparse Core Ops, SparseCore 0:
  10.2 50.2 all-gather.9
  62.6 41.5 all-gather.11
  106.4 53.3 all-gather.7
  161.9 48.2 all-gather.13
  212.2 79.8 all-gather.15
  294.3 79.3 all-gather.17
  375.9 79.3 all-gather.19
  624.6 59.2 reduce-scatter.9
  687.7 60.7 reduce-scatter.11
  752.2 71.7 reduce-scatter.13
  827.9 71.8 reduce-scatter.7
  903.7 193.0 reduce-scatter.15
  1100.9 193.1 reduce-scatter.17
  1298.0 193.1 reduce-scatter.19
  1494.1 110.0 all-reduce.18
